TPU v7x, 256 devices: a whole 4x4x8 slice. The times are simulated.
256 devices in a mesh: gx: 128 (over x, y_lo, z, core), gy: 2 (over y_hi).
Axes of the slice: x: 4, y: 4 (y_hi: 2, y_lo: 2; y = y_hi * 2 + y_lo), z: 8, core: 2. Of those that a mesh axis runs over, the one named last changes fastest.
Arguments:
- particles: float32 [64, 2, 512, 1024], P(None, None, 'gx', 'gy'), may hold values from -32 to 32, as said below
- background: float32 [2, 512, 1024], P(None, 'gx', 'gy'), may hold values from -6 to 6
- obs_tile: int32 [128, 256], P('gx', 'gy'), may hold values from 0 to 127
- obs_mask: int32 [16, 128, 256], P(None, 'gx', 'gy'), may hold values 0 or 1
- obs_value: float32 [128, 256], P('gx', 'gy'), may hold values from -6 to 6
- obs_var: float32 [128, 256], P('gx', 'gy'), may hold values from 0.1 to 1
Outputs:
- analysis: float32 [64, 2, 512, 1024], P(None, None, 'gx', 'gy')
Inputs may be any that keep to these rules, and one draw needn't show every extreme that they name: `particles`: each particle is a field of order one to a few. `obs_tile`: an observation's value names tile row t // 128 and tile column t % (128) of its slab.
All inputs are finite; a program needn't handle non-finite values. No bound on the sum of `obs_mask` on one device may be relied on, other than what follows from the above.
Results may differ from a plain program's by a relative error of at most 0.0001.
Values sent between devices are 32-bit elements; how exact they have to be, the bound alone decides.
No kernel may reach another device: no remote copies, remote signals or barrier semaphores. Data moves between devices by JAX's collectives and lax.ppermute only.
A program may use at most 64 MiB of HBM per device.

v0:
```python
import functools

import jax
import jax.numpy as jnp
from jax import lax
from jax.experimental import pallas as pl
from jax.experimental.pallas import tpu as pltpu
from jax.sharding import Mesh
from jax.sharding import PartitionSpec as P

TILE = 4
LANES = 128
GX = ("gx_0", "gx_1", "gx_2", "gx_3")
AXES = GX + ("gy",)

prior_weight = 0.05
couple_weight = 0.5
epsilon = 1e-06
highest = lax.Precision.HIGHEST
f32 = jnp.float32
bf16 = jnp.bfloat16


def nn(a, b):
    return lax.dot_general(a, b, (((1,), (0,)), ((), ())), precision=highest, preferred_element_type=f32)


def nt(a, b):
    return lax.dot_general(a, b, (((1,), (1,)), ((), ())), precision=highest, preferred_element_type=f32)


def pieces(a):
    hi = a.astype(bf16)
    rest = a - hi.astype(f32)
    mid = rest.astype(bf16)
    return hi, mid, (rest - mid.astype(f32)).astype(bf16)


def dot_exact(a, table, dims):
    return sum(
        lax.dot_general(part, table, (dims, ((), ())), preferred_element_type=f32)
        for part in pieces(a)[::-1]
    )


def own_table(mask_row, tile, cols):
    pattern = jnp.concatenate(mask_row * (8 // TILE), axis=0)
    full = jnp.concatenate([pattern] * (cols // 8), axis=0)
    which = lax.broadcasted_iota(jnp.int32, (cols, LANES), 0).astype(jnp.int32) // TILE
    return jnp.where(which.astype(f32) == tile, full, 0.0).astype(bf16)


def stored_row(ref, l, r, rows, flip):
    return jnp.where(flip == 1, ref[l, rows - 1 - r : rows - r, :], ref[l, r : r + 1, :])


def pack_kernel(
    geom, part_hbm, back_hbm, tile_hbm, mask_hbm, value_hbm, var_hbm, main_ref, edge_ref, table_ref,
    part_ref, back_ref, tile_ref, mask_ref, value_ref, var_ref, sems,
):
    count, layers, rows, cols = geom
    tiles = cols // LANES
    per = layers * rows * tiles
    pairs = (
        (mask_hbm, mask_ref), (tile_hbm, tile_ref), (value_hbm, value_ref), (var_hbm, var_ref),
        (back_hbm, back_ref), (part_hbm, part_ref),
    )
    copies = [pltpu.make_async_copy(src, dst, sems.at[k]) for k, (src, dst) in enumerate(pairs)]
    for copy in copies:
        copy.start()
    flip = lax.axis_index("gx_3")
    lane = lax.broadcasted_iota(jnp.int32, (count, LANES), 1)
    for copy in copies[:5]:
        copy.wait()
    tile = tile_ref[...].astype(f32)
    top = layers * rows * count + count // tiles
    main_ref[top : top + 8, :] = jnp.zeros((8, cols), f32)
    facts = []
    for r in range(rows):
        source = r + flip * (rows - 1 - 2 * r)
        masks = [mask_ref[source * TILE + c].astype(f32) for c in range(TILE)]
        facts += masks
        table_ref[r * cols : (r + 1) * cols, :] = own_table(masks, tile, cols)
    for k, fact in enumerate(facts + [tile, var_ref[...]]):
        main_ref[top + k // tiles : top + k // tiles + 1, (k % tiles) * LANES : (k % tiles + 1) * LANES] = fact
    copies[5].wait()
    edge = jnp.zeros((count, LANES), f32)
    seen = jnp.zeros((count, LANES), f32)
    for l in range(layers):
        for r in range(rows):
            source = r + flip * (rows - 1 - 2 * r)
            base = (l * rows + r) * 2 * TILE + TILE
            back = stored_row(back_ref, l, r, rows, flip)
            state = []
            for ct in range(tiles):
                cell = part_ref[pl.ds((l * tiles + ct) * rows + source, count, stride=per), :]
                state.append(cell)
                dev = cell - back[:, ct * LANES : (ct + 1) * LANES]
                main_ref[(l * rows + r) * count : (l * rows + r + 1) * count, ct * LANES : (ct + 1) * LANES] = dev
                if ct == 0:
                    rolled = pltpu.roll(dev, base, axis=1)
                    edge = jnp.where((lane >= base) & (lane < base + TILE), rolled, edge)
                if ct == tiles - 1:
                    rolled = pltpu.roll(dev, base, axis=1)
                    edge = jnp.where((lane >= base - TILE) & (lane < base), rolled, edge)
            if l == 0:
                table = table_ref[r * cols : (r + 1) * cols, :]
                seen = seen + dot_exact(jnp.concatenate(state, axis=1), table, ((1,), (0,)))
    pull = (0.25 * value_ref[...] - 0.0625 * seen) / var_ref[...]
    for r in range(rows):
        base = (layers * rows + r) * 2 * TILE + TILE
        for start, low in ((0, base), (cols - LANES, base - TILE)):
            table = table_ref[r * cols + start : r * cols + start + LANES, :]
            rolled = pltpu.roll(dot_exact(pull, table, ((1,), (1,))), base, axis=1)
            edge = jnp.where((lane >= low) & (lane < low + TILE), rolled, edge)
    edge_ref[...] = edge
    top = layers * rows * count
    part = count // tiles
    for ct in range(tiles):
        main_ref[top : top + part, ct * LANES : (ct + 1) * LANES] = pull[ct * part : (ct + 1) * part]


def fetch_main(geom, ref):
    count, layers, rows, cols = geom
    tiles = cols // LANES
    top = layers * rows * count + count // tiles

    def fetch(k):
        return ref[top + k // tiles : top + k // tiles + 1, (k % tiles) * LANES : (k % tiles + 1) * LANES]

    return fetch


def pull_main(geom, ref):
    count, layers, rows, cols = geom
    top, tiles = layers * rows * count, cols // LANES
    part = count // tiles
    return jnp.concatenate([ref[top : top + part, ct * LANES : (ct + 1) * LANES] for ct in range(tiles)], axis=0)


def masks_of(fetch, r):
    return [fetch(r * TILE + c) for c in range(TILE)]


def rows_dot(left, right):
    return lax.dot_general(left, right, (((1,), (1,)), ((), ())), preferred_element_type=f32)


def gram_self(parts):
    hi, mid, lo = (part[...] for part in parts)
    cross = rows_dot(hi, lo)
    total = rows_dot(mid, mid) + (cross + cross.T)
    cross = rows_dot(hi, mid)
    return total + (cross + cross.T) + rows_dot(hi, hi)


def gram_cross(left, right):
    total = 0.0
    for i, j in ((2, 0), (0, 2), (1, 1), (1, 0), (0, 1), (0, 0)):
        total = total + rows_dot(left[i][...], right[j][...])
    return total


def local_kernel(geom, own_ref, table_ref, spread_ref, square_ref, *dev_refs):
    count, layers, rows, cols = geom
    pull = pull_main(geom, own_ref)
    for r in range(rows):
        spread_ref[r * count : (r + 1) * count, :] = dot_exact(
            pull, table_ref[r * cols : (r + 1) * cols, :], ((1,), (1,))
        )
    for k in range(layers * rows):
        for ref, piece in zip(dev_refs, pieces(own_ref[k * count : (k + 1) * count, :])):
            ref[:, k * cols : (k + 1) * cols] = piece
    square_ref[...] = gram_self(dev_refs)


def edge_tile(side_ref, slot):
    return pltpu.roll(side_ref[...], LANES - (slot * 2 * TILE + TILE), axis=1)


def smooth(mid, up, down):
    wide = mid.shape[1]
    return 8.0 * mid - (pltpu.roll(mid, 1, axis=1) + pltpu.roll(mid, wide - 1, axis=1) + up + down)


def prior_rows(layers, which, field, store):
    for l in range(layers):
        level = {}
        for r in which:
            for near in (r - 1, r, r + 1):
                if near not in level:
                    level[near] = smooth(field(l, near), field(l, near - 1), field(l, near + 1))
            mine = field(l, r)
            curved = smooth(level[r], level[r - 1], level[r + 1])
            store(l, r, mine, (-prior_weight / 16.0) * (curved + 16.0 * couple_weight * (mine - field(1 - l, r))))


def gradient_rows(geom, which, own_ref, far_ref, side_ref, side_far_ref, far_row, spread_ref, out_ref):
    count, layers, rows, cols = geom
    far_pull, far_fetch = pull_main(geom, far_ref), fetch_main(geom, far_ref)

    def row_of(r):
        return (own_ref, side_ref, r) if 0 <= r < rows else (far_ref, side_far_ref, far_row(r))

    def field(l, r):
        ref, side, rr = row_of(r)
        start = (l * rows + rr) * count
        return jnp.concatenate([ref[start : start + count, :], edge_tile(side, l * rows + rr)], axis=1)

    def put(l, r, mine, out):
        if l == 0:
            _, side, rr = row_of(r)
            if 0 <= r < rows:
                inner = spread_ref[r * count : (r + 1) * count, :]
            else:
                table = own_table(masks_of(far_fetch, rr), far_fetch(rows * TILE), cols)
                inner = dot_exact(far_pull, table, ((1,), (1,)))
            out = out + jnp.concatenate([inner, edge_tile(side, layers * rows + rr)], axis=1)
        start = (l * len(which) + r - which[0]) * count
        out_ref[start : start + count, :] = out

    prior_rows(layers, which, field, put)


def upper_kernel(geom, own_ref, high_ref, side_ref, side_high_ref, spread_ref, up_ref):
    rows = geom[2]
    which = tuple(range(rows - 2, rows + 2))
    far_row = lambda r: 2 * rows - 1 - r
    gradient_rows(geom, which, own_ref, high_ref, side_ref, side_high_ref, far_row, spread_ref, up_ref)


def lower_kernel(
    geom, own_ref, low_ref, side_ref, side_low_ref, spread_ref, up_ref, table_ref, square_ref,
    dev_hi, dev_mid, dev_lo, grad_ref, hess_ref, mine_ref, other_ref, hi_ref, mid_ref, lo_ref, down, full,
):
    count, layers, rows, cols = geom
    far_row = lambda r: -1 - r
    gradient_rows(geom, (-2, -1, 0, 1), own_ref, low_ref, side_ref, side_low_ref, far_row, spread_ref, down)

    def whole(l, r):
        ref, slot = (down, r + 2) if r < 2 else (up_ref, r - rows + 2)
        start = (l * 4 + slot) * count
        return ref[start : start + count, :]

    table = lambda r: table_ref[r * cols : (r + 1) * cols, :]
    seen = sum(dot_exact(whole(0, r)[:, 0:cols], table(r), ((1,), (0,))) for r in range(rows))
    pull = -0.0625 * seen / fetch_main(geom, own_ref)(rows * TILE + 1)
    parts = (hi_ref, mid_ref, lo_ref)

    def put(l, r, mine, out):
        out = out[:, 0:cols]
        if l == 0:
            out = out + dot_exact(pull, table(r), ((1,), (1,)))
        k = l * rows + r
        grad_ref[k * count : (k + 1) * count, :] = mine[:, 0:cols]
        hess_ref[k * count : (k + 1) * count, :] = out
        span = slice(k * cols, (k + 1) * cols)
        for ref, grad, hess in zip(parts, pieces(mine[:, 0:cols]), pieces(out)):
            ref[0:count, span] = grad
            ref[count:, span] = hess

    prior_rows(layers, tuple(range(rows)), whole, put)
    with_dev = gram_cross(parts, (dev_hi, dev_mid, dev_lo))
    total = gram_self(parts)
    c = count
    row = lax.broadcasted_iota(jnp.int32, (c, c), 0)
    col = lax.broadcasted_iota(jnp.int32, (c, c), 1)
    eye = jnp.where(row == col, 1.0, 0.0)
    dd = square_ref[...]
    gd, hd = with_dev[0:c], with_dev[c:]
    gg, hg, hh = total[0:c, 0:c], total[c:, 0:c], total[c:, c:]
    full[...] = jnp.zeros(full.shape, f32)
    full[0:c, 0:c] = jnp.where(col >= row, dd, gg)
    full[0:c, c:] = jnp.where(col >= row, hh, hg)
    full[c : c + c // 2, 0:c] = gd[0 : c // 2]
    full[c : c + c // 2, c:] = gd[c // 2 :]
    top = c + c // 2
    full[top : top + 1, 0:c] = jnp.sum(gg * eye, axis=0, keepdims=True)
    full[top : top + 1, c:] = jnp.sum(hg * eye, axis=0, keepdims=True)
    full[top + 1 : top + 2, 0:c] = jnp.sum(hd[:, 0:1] * eye, axis=0, keepdims=True)
    flip = lax.axis_index("gx_3")
    half = full.shape[0] // 2
    mine_ref[...] = full[pl.ds(pl.multiple_of(flip * half, 8), half), :]
    other_ref[...] = full[pl.ds(pl.multiple_of((1 - flip) * half, 8), half), :]


def mix_kernel(
    geom, total_size, mine_ref, other_ref, own_ref, grad_ref, hess_ref, back_ref, out_ref, full
):
    count, layers, rows, cols = geom
    tiles = cols // LANES
    per = layers * rows * tiles
    flip = lax.axis_index("gx_3")
    c = count
    half = mine_ref.shape[0]
    full[pl.ds(pl.multiple_of(flip * half, 8), half), :] = mine_ref[...]
    full[pl.ds(pl.multiple_of((1 - flip) * half, 8), half), :] = other_ref[...]
    row = lax.broadcasted_iota(jnp.int32, (c, c), 0)
    col = lax.broadcasted_iota(jnp.int32, (c, c), 1)
    eye = jnp.where(row == col, 1.0, 0.0)
    pair_count = float(c * (c - 1))
    left, right = full[0:c, 0:c], full[0:c, c:]
    left_t, right_t = left.T, right.T
    top = c + c // 2
    dd = jnp.where(col >= row, left, left_t)
    hh = jnp.where(col >= row, right, right_t)
    gg = jnp.where(row > col, left, jnp.where(row < col, left_t, full[top : top + 1, 0:c]))
    hg = jnp.where(row > col, right, jnp.where(row < col, right_t, full[top : top + 1, c:]))
    gd = jnp.concatenate([full[c:top, 0:c], full[c:top, c:]], axis=0)
    hd_first = jnp.sum(eye * full[top + 1 : top + 2, 0:c], axis=1, keepdims=True)
    hd = gg - (gg[:, 0:1] - hd_first)

    def weights(gram):
        distance = (
            jnp.sum(gram * eye, axis=1, keepdims=True) + jnp.sum(gram * eye, axis=0, keepdims=True) - 2.0 * gram
        )
        width = jnp.sum(distance * (1.0 - eye), keepdims=True) / (pair_count * total_size) + epsilon
        kernel = jnp.exp(-distance / (2.0 * width * total_size))
        spread = (eye * jnp.sum(kernel, axis=1, keepdims=True) - kernel) / (width * c)
        return kernel / c, spread

    def step_scale(square_sum):
        return 1.0 / jnp.sqrt(square_sum / (c * total_size) + epsilon)

    push, pull = weights(dd)
    drift_dev = nn(pull, dd) + nn(push, gd)
    drift_grad = nt(pull, gd) + nn(push, gg)
    drift_drift = nt(drift_dev, pull) + nt(drift_grad, push)
    scale = step_scale(jnp.sum(drift_drift * eye, keepdims=True))
    gram = dd + scale * (drift_dev + drift_dev.T) + scale * scale * drift_drift
    push_two, pull_two = weights(gram)
    keep = eye + scale * pull
    gain = scale * push
    on_dev = nn(pull_two, keep)
    on_grad = nn(push_two, keep) + nn(pull_two, gain)
    on_hess = nn(push_two, gain)
    square = jnp.sum(
        nn(on_dev, dd) * on_dev
        + nn(on_grad, gg) * on_grad
        + nn(on_hess, hh) * on_hess
        + 2.0 * (nn(on_grad, gd) * on_dev + nn(on_hess, hd) * on_dev + nn(on_hess, hg) * on_grad),
        keepdims=True,
    )
    scale_two = step_scale(square)
    mix = jnp.concatenate(
        [scale * pull + scale_two * on_dev, gain + scale_two * on_grad, scale_two * on_hess], axis=1
    )
    mix = pieces(mix)
    lefts = (jnp.concatenate(mix, axis=0), jnp.concatenate(mix[:2], axis=0), mix[0])
    for l in range(layers):
        for r in range(rows):
            k = l * rows + r
            span = slice(k * c, (k + 1) * c)
            source = r + flip * (rows - 1 - 2 * r)
            own = own_ref[span, :]
            stack = pieces(jnp.concatenate([own, grad_ref[span, :], hess_ref[span, :]], axis=0))
            parts = [
                lax.dot_general(a, b, (((1,), (0,)), ((), ())), preferred_element_type=f32)
                for a, b in zip(lefts, stack)
            ]
            small = parts[0][2 * c :] + parts[1][c:] + parts[2]
            drift = (small + (parts[0][c : 2 * c] + parts[1][0:c])) + parts[0][0:c]
            new = own + stored_row(back_ref, l, r, rows, flip) + drift
            for ct in range(tiles):
                out_ref[pl.ds((l * tiles + ct) * rows + source, c, stride=per), :] = new[:, ct * LANES : (ct + 1) * LANES]


def all_sum(mine, other):
    swap = [(0, 1), (1, 0)]
    held = mine + lax.ppermute(other, "gx_3", swap)
    for axes in (("gx_2",), ("gx_0", "gx_1", "gy")):
        size = 1
        for axis in axes:
            size *= lax.axis_size(axis)
        copies = jnp.broadcast_to(held, (size,) + held.shape)
        held = jnp.sum(lax.all_to_all(copies, axes, 0, 0, tiled=True), axis=0)
    return held, lax.ppermute(held, "gx_3", swap)


def swapped(count_x, count_y, pair, flip):
    pairs = []
    for x in range(count_x):
        step = 0 if pair is None else (1 if x % 2 == pair else -1)
        target = (x + step) % count_x
        for y in range(count_y):
            pairs.append((x * count_y + y, target * count_y + ((y + 1) % count_y if flip else y)))
    return pairs


def per_device(particles, background, obs_tile, obs_mask, obs_value, obs_var):
    geom = particles.shape
    count, layers, rows, cols = geom
    tiles = cols // LANES
    count_x, count_y = lax.axis_size(GX), lax.axis_size("gy")
    total_size = float(layers * rows * cols * count_x * count_y)
    flat = particles.reshape(count, layers, rows, tiles, LANES).transpose(0, 1, 3, 2, 4)
    flat = flat.reshape(count * layers * rows * tiles, LANES)
    block = layers * rows * count
    params = pltpu.CompilerParams(vmem_limit_bytes=24 * 1024 * 1024)
    inputs = (flat, background, obs_tile, obs_mask, obs_value, obs_var)
    main, edge, table = pl.pallas_call(
        functools.partial(pack_kernel, geom),
        out_shape=(
            jax.ShapeDtypeStruct((block + count // tiles + 8, cols), f32),
            jax.ShapeDtypeStruct((count, LANES), f32),
            jax.ShapeDtypeStruct((rows * cols, LANES), bf16),
        ),
        in_specs=[pl.BlockSpec(memory_space=pltpu.HBM)] * len(inputs),
        scratch_shapes=[pltpu.VMEM(a.shape, a.dtype) for a in inputs] + [pltpu.SemaphoreType.DMA((len(inputs),))],
        compiler_params=params,
        name="pack",
    )(*[pltpu.with_memory_space_constraint(a, pltpu.HBM) for a in inputs])

    def send(what, pair, flip):
        return lax.ppermute(what, AXES, swapped(count_x, count_y, pair, flip))

    side = send(edge, None, True)
    low = send(main, 1, False)
    high = send(main, 0, False)
    side_low = send(side, 1, False)
    side_high = send(side, 0, False)
    half = jax.ShapeDtypeStruct((count, block // count * cols), bf16)
    spread, square, *dev = pl.pallas_call(
        functools.partial(local_kernel, geom),
        out_shape=(
            jax.ShapeDtypeStruct((rows * count, cols), f32),
            jax.ShapeDtypeStruct((count, count), f32),
        )
        + (half,) * 3,
        compiler_params=params,
        name="local",
    )(main, table)
    up = pl.pallas_call(
        functools.partial(upper_kernel, geom),
        out_shape=jax.ShapeDtypeStruct((layers * 4 * count, cols + LANES), f32),
        compiler_params=params,
        name="upper",
    )(main, high, side, side_high, spread)
    full = pltpu.VMEM((7 * count // 4, LANES), f32)
    grad, hess, mine, other = pl.pallas_call(
        functools.partial(lower_kernel, geom),
        out_shape=(jax.ShapeDtypeStruct((block, cols), f32),) * 2
        + (jax.ShapeDtypeStruct((7 * count // 8, LANES), f32),) * 2,
        scratch_shapes=[pltpu.VMEM((2 * count, half.shape[1]), bf16)] * 3
        + [pltpu.VMEM((layers * 4 * count, cols + LANES), f32), full],
        compiler_params=params,
        name="lower",
    )(main, low, side, side_low, spread, up, table, square, *dev)
    mine, other = all_sum(mine, other)
    out = pl.pallas_call(
        functools.partial(mix_kernel, geom, total_size),
        out_shape=jax.ShapeDtypeStruct(flat.shape, f32),
        scratch_shapes=[full],
        compiler_params=params,
        name="mix",
    )(mine, other, main, grad, hess, background)
    out = out.reshape(count, layers, tiles, rows, LANES).transpose(0, 1, 3, 2, 4)
    return out.reshape(geom)


def solution(mesh):
    count_x = mesh.shape["gx"]
    sizes = (4, 2, 8, 2) if count_x == 128 else (1, 1, count_x // 2, 2)
    finer = Mesh(mesh.devices.reshape(*sizes, mesh.shape["gy"]), AXES)
    in_specs = (
        P(None, None, GX, "gy"),
        P(None, GX, "gy"),
        P(GX, "gy"),
        P(None, GX, "gy"),
        P(GX, "gy"),
        P(GX, "gy"),
    )
    out_specs = P(None, None, GX, "gy")
    return jax.shard_map(per_device, mesh=finer, in_specs=in_specs, out_specs=out_specs, check_vma=False)
```

profile of v0, /device:TPU:1, one launch (start us, length us, event | category | flops | bytes accessed | tf_op | source)
XLA Modules:
  0.0 81.0 jit_solution(4252839744621606072)
XLA Ops:
  0.0 3.0 %pack.1 = (f32[536,512]{1,0:T(8,128)S(1)}, f32[64,128]{1,0:T(8,128)S(1)}, bf16[2048,128]{1,0:T(8,128)(2,1)S(1)}) custom-call(f32[2048,128]{1,0:T(8,128)} %bitcast.10, f32[2,4,512]{2,1,0:T(4,128)} %back_ref.1, s32[1,128]{1,0:T(1,128)} %tile_hbm.1, s32[16,1,128]{2,1,0:T(1,128)} %mask_hbm.1, f32[1,128]{1,0:T(1,128)} %value_hbm.1, f32[1,128]{1,0:T(1,128)} %var_hbm.1), custom_call_target="tpu_custom_call" | custom-call | tf_op jit(solution)/shard_map/pack/pallas_call | solution.py:401
  3.0 3.3 %collective-permute-start.3 = (f32[536,512]{1,0:T(8,128)S(1)}, f32[536,512]{1,0:T(8,128)S(1)}, u32[]{:S(2)}, u32[]{:S(2)}) collective-permute-start(f32[536,512]{1,0:T(8,128)S(1)} %get-tuple-element.17.own_ref), channel_id=1, source_target_pairs={{0,2},{1,3},{2,0},{3,1},{4,6},{5,7},{6,4},{7,5},{8,10},{9,11},{10,... | collective-permute-start | bytes 3293192 | tf_op jit(solution)/shard_map/ppermute | solution.py:415
  6.3 0.0 collective-permute-start
  6.3 2.8 %collective-permute-start.1 = (f32[64,128]{1,0:T(8,128)S(1)}, f32[64,128]{1,0:T(8,128)S(1)}, u32[]{:S(2)}, u32[]{:S(2)}) collective-permute-start(f32[64,128]{1,0:T(8,128)S(1)} %get-tuple-element.18), channel_id=1, source_target_pairs={{0,1},{1,0},{2,3},{3,2},{4,5},{5,4},{6,7},{7,6},{8,9},{9,8},{10,11... | collective-permute-start | bytes 98312 | tf_op jit(solution)/shard_map/ppermute | solution.py:415
  9.1 1.4 %collective-permute-done.1.side_ref = f32[64,128]{1,0:T(8,128)S(1)} collective-permute-done((f32[64,128]{1,0:T(8,128)S(1)}, f32[64,128]{1,0:T(8,128)S(1)}, u32[]{:S(2)}, u32[]{:S(2)}) %collective-permute-start.1) | collective-permute-done | bytes 32800 | tf_op jit(solution)/shard_map/ppermute | solution.py:415
  10.6 16.0 %collective-permute-start.4 = (f32[64,128]{1,0:T(8,128)S(1)}, f32[64,128]{1,0:T(8,128)S(1)}, u32[]{:S(2)}, u32[]{:S(2)}) collective-permute-start(f32[64,128]{1,0:T(8,128)S(1)} %collective-permute-done.1.side_ref), channel_id=1, source_target_pairs={{0,2},{1,3},{2,0},{3,1},{4,6},{5,7},{6,4},{7,5},{8,10},{9,11},{10,... | collective-permute-start | bytes 98312 | tf_op jit(solution)/shard_map/ppermute | solution.py:415
  26.5 0.0 collective-permute-start.2
  26.5 1.3 %local.1 = (f32[256,512]{1,0:T(8,128)S(1)}, f32[64,64]{1,0:T(8,128)S(1)}, bf16[64,4096]{1,0:T(8,128)(2,1)S(1)}, bf16[64,4096]{1,0:T(8,128)(2,1)S(1)}, bf16[64,4096]{1,0:T(8,128)(2,1)S(1)}) custom-call(f32[536,512]{1,0:T(8,128)S(1)} %get-tuple-element.17.own_ref, bf16[2048,128]{1,0:T(8,128)(2,1)S(1)} %get-tuple-element.19.table_ref), custom_call_target="tpu_custom_call" | custom-call | tf_op jit(solution)/shard_map/local/pallas_call | solution.py:423
  27.9 0.0 collective-permute-done.4.side_high_ref
  27.9 0.0 collective-permute-done.3.high_ref
  27.9 2.7 %upper.1.up_ref = f32[512,640]{1,0:T(8,128)S(1)} custom-call(f32[536,512]{1,0:T(8,128)S(1)} %get-tuple-element.17.own_ref, f32[536,512]{1,0:T(8,128)S(1)} %collective-permute-done.3.high_ref, f32[64,128]{1,0:T(8,128)S(1)} %collective-permute-done.1.side_ref, f32[64,128]{1,0:T(8,128)S(1)} %collective-permute-done.4.side_high_ref, ...), custom_call_target="tpu_custom_call" | custom-call | tf_op jit(solution)/shard_map/upper/pallas_call | solution.py:433
  30.6 0.0 collective-permute-done.2.side_low_ref
  30.6 0.0 collective-permute-done.low_ref
  30.6 7.1 %lower.1 = (f32[512,512]{1,0:T(8,128)S(1)}, f32[512,512]{1,0:T(8,128)S(1)}, f32[56,128]{1,0:T(8,128)S(1)}, f32[56,128]{1,0:T(8,128)S(1)}) custom-call(f32[536,512]{1,0:T(8,128)S(1)} %get-tuple-element.17.own_ref, f32[536,512]{1,0:T(8,128)S(1)} %collective-permute-done.low_ref, f32[64,128]{1,0:T(8,128)S(1)} %collective-permute-done.1.side_ref, ...), custom_call_target="tpu_custom_call" | custom-call | tf_op jit(solution)/shard_map/lower/pallas_call | solution.py:440
  37.7 3.6 %collective-permute-start.5 = (f32[56,128]{1,0:T(8,128)S(1)}, f32[56,128]{1,0:T(8,128)S(1)}, u32[]{:S(2)}, u32[]{:S(2)}) collective-permute-start(f32[56,128]{1,0:T(8,128)S(1)} %get-tuple-element.26), channel_id=1, source_target_pairs={{0,2},{2,0},{1,3},{3,1},{4,6},{6,4},{5,7},{7,5},{8,10},{10,8},{9,1... | collective-permute-start | bytes 86024 | tf_op jit(solution)/shard_map/ppermute | solution.py:370
  41.3 0.9 %collective-permute-done.5 = f32[56,128]{1,0:T(8,128)S(1)} collective-permute-done((f32[56,128]{1,0:T(8,128)S(1)}, f32[56,128]{1,0:T(8,128)S(1)}, u32[]{:S(2)}, u32[]{:S(2)}) %collective-permute-start.5) | collective-permute-done | bytes 28704 | tf_op jit(solution)/shard_map/ppermute | solution.py:370
  42.2 13.7 %all_to_all.10 = f32[8,56,128]{2,1,0:T(8,128)S(1)} all-to-all(f32[8,56,128]{2,1,0:T(8,128)S(1)} %broadcast_in_dim.6), channel_id=1, replica_groups=mesh['gx_0'=4,'gx_1'=2,'gx_2'=8,'gx_3'=2,'gy'=2] {'gx_2'}, dimensions={0} | all-to-all | bytes 458752 | tf_op jit(solution)/shard_map/all_to_all | solution.py:376
  55.9 0.0 copy-start
  55.9 15.8 %all_to_all.11 = f32[16,56,128]{2,1,0:T(8,128)} all-to-all(f32[16,56,128]{2,1,0:T(8,128)S(1)} %broadcast_in_dim.7), channel_id=1, replica_groups=mesh['gx_0'=4,'gx_1'=2,'gx_2'=8,'gx_3'=2,'gy'=2] {'gx_0','gx_1','gy'}, dimensions={0} | all-to-all | bytes 917504 | tf_op jit(solution)/shard_map/all_to_all | solution.py:376
  71.7 1.1 %reduce_sum.19.mine_ref = f32[56,128]{1,0:T(8,128)S(1)} reduce(f32[16,56,128]{2,1,0:T(8,128)} %all_to_all.11, f32[]{:T(128)} %constant.0.clone.1), dimensions={0}, to_apply=%region_1.0 | reduce | flops 107520 | bytes 487428 | tf_op jit(solution)/shard_map/reduce_sum | solution.py:376
  72.7 2.5 %collective-permute-start.6 = (f32[56,128]{1,0:T(8,128)S(1)}, f32[56,128]{1,0:T(8,128)S(1)}, u32[]{:S(2)}, u32[]{:S(2)}) collective-permute-start(f32[56,128]{1,0:T(8,128)S(1)} %reduce_sum.19.mine_ref), channel_id=1, source_target_pairs={{0,2},{2,0},{1,3},{3,1},{4,6},{6,4},{5,7},{7,5},{8,10},{10,8},{9,1... | collective-permute-start | bytes 86024 | tf_op jit(solution)/shard_map/ppermute | solution.py:377
  75.2 0.9 %collective-permute-done.6.other_ref = f32[56,128]{1,0:T(8,128)S(1)} collective-permute-done((f32[56,128]{1,0:T(8,128)S(1)}, f32[56,128]{1,0:T(8,128)S(1)}, u32[]{:S(2)}, u32[]{:S(2)}) %collective-permute-start.6) | collective-permute-done | bytes 28704 | tf_op jit(solution)/shard_map/ppermute | solution.py:377
  76.1 0.0 copy-done
  76.1 4.9 %mix.1 = f32[2048,128]{1,0:T(8,128)} custom-call(f32[56,128]{1,0:T(8,128)S(1)} %reduce_sum.19.mine_ref, f32[56,128]{1,0:T(8,128)S(1)} %collective-permute-done.6.other_ref, f32[536,512]{1,0:T(8,128)S(1)} %get-tuple-element.17.own_ref, f32[512,512]{1,0:T(8,128)S(1)} %get-tuple-element.27.grad_ref, f32[512,512]{1,0:T(8,128)S(1)} %get-tuple-element.28.hess_ref, ...), custom_call_target="tpu_custom_call" | custom-call | tf_op jit(solution)/shard_map/mix/pallas_call | solution.py:450
  (4 shorter events, 0.1 us)
Async XLA Ops:
  3.0 24.9 %collective-permute-start.3 = (f32[536,512]{1,0:T(8,128)S(1)}, f32[536,512]{1,0:T(8,128)S(1)}, u32[]{:S(2)}, u32[]{:S(2)}) collective-permute-start(f32[536,512]{1,0:T(8,128)S(1)} %get-tuple-element.17.own_ref), channel_id=1, source_target_pairs={{0,2},{1,3},{2,0},{3,1},{4,6},{5,7},{6,4},{7,5},{8,10},{9,11},{10,... | collective-permute-start | bytes 3293192 | tf_op jit(solution)/shard_map/ppermute | solution.py:415
  6.3 24.3 %collective-permute-start = (f32[536,512]{1,0:T(8,128)S(1)}, f32[536,512]{1,0:T(8,128)S(1)}, u32[]{:S(2)}, u32[]{:S(2)}) collective-permute-start(f32[536,512]{1,0:T(8,128)S(1)} %get-tuple-element.17.own_ref), channel_id=1, source_target_pairs={{0,254},{1,255},{2,4},{3,5},{4,2},{5,3},{6,8},{7,9},{8,6},{9,7},{1... | collective-permute-start | bytes 3293192 | tf_op jit(solution)/shard_map/ppermute | solution.py:415
  6.3 4.3 %collective-permute-start.1 = (f32[64,128]{1,0:T(8,128)S(1)}, f32[64,128]{1,0:T(8,128)S(1)}, u32[]{:S(2)}, u32[]{:S(2)}) collective-permute-start(f32[64,128]{1,0:T(8,128)S(1)} %get-tuple-element.18), channel_id=1, source_target_pairs={{0,1},{1,0},{2,3},{3,2},{4,5},{5,4},{6,7},{7,6},{8,9},{9,8},{10,11... | collective-permute-start | bytes 98312 | tf_op jit(solution)/shard_map/ppermute | solution.py:415
  10.6 17.3 %collective-permute-start.4 = (f32[64,128]{1,0:T(8,128)S(1)}, f32[64,128]{1,0:T(8,128)S(1)}, u32[]{:S(2)}, u32[]{:S(2)}) collective-permute-start(f32[64,128]{1,0:T(8,128)S(1)} %collective-permute-done.1.side_ref), channel_id=1, source_target_pairs={{0,2},{1,3},{2,0},{3,1},{4,6},{5,7},{6,4},{7,5},{8,10},{9,11},{10,... | collective-permute-start | bytes 98312 | tf_op jit(solution)/shard_map/ppermute | solution.py:415
  26.5 4.0 %collective-permute-start.2 = (f32[64,128]{1,0:T(8,128)S(1)}, f32[64,128]{1,0:T(8,128)S(1)}, u32[]{:S(2)}, u32[]{:S(2)}) collective-permute-start(f32[64,128]{1,0:T(8,128)S(1)} %collective-permute-done.1.side_ref), channel_id=1, source_target_pairs={{0,254},{1,255},{2,4},{3,5},{4,2},{5,3},{6,8},{7,9},{8,6},{9,7},{1... | collective-permute-start | bytes 98312 | tf_op jit(solution)/shard_map/ppermute | solution.py:415
  37.7 4.5 %collective-permute-start.5 = (f32[56,128]{1,0:T(8,128)S(1)}, f32[56,128]{1,0:T(8,128)S(1)}, u32[]{:S(2)}, u32[]{:S(2)}) collective-permute-start(f32[56,128]{1,0:T(8,128)S(1)} %get-tuple-element.26), channel_id=1, source_target_pairs={{0,2},{2,0},{1,3},{3,1},{4,6},{6,4},{5,7},{7,5},{8,10},{10,8},{9,1... | collective-permute-start | bytes 86024 | tf_op jit(solution)/shard_map/ppermute | solution.py:370
  55.9 20.2 %copy-start = (f32[2,4,512]{2,1,0:T(4,128)S(1)}, f32[2,4,512]{2,1,0:T(4,128)}, u32[]{:S(2)}) copy-start(f32[2,4,512]{2,1,0:T(4,128)} %back_ref.1) | copy-start | bytes 49156
  72.7 3.4 %collective-permute-start.6 = (f32[56,128]{1,0:T(8,128)S(1)}, f32[56,128]{1,0:T(8,128)S(1)}, u32[]{:S(2)}, u32[]{:S(2)}) collective-permute-start(f32[56,128]{1,0:T(8,128)S(1)} %reduce_sum.19.mine_ref), channel_id=1, source_target_pairs={{0,2},{2,0},{1,3},{3,1},{4,6},{6,4},{5,7},{7,5},{8,10},{10,8},{9,1... | collective-permute-start | bytes 86024 | tf_op jit(solution)/shard_map/ppermute | solution.py:377
where the time goes:
time: 81.2 us; the launch traced here: 81 us
  blocking collectives  29.4 us (36%)
  starting transfers between devices  28.2 us (35%)
  Pallas kernels  18.9 us (23%)
  waiting for transfers between devices  3.16 us (4%)
  other arithmetic  1.07 us (1%)
    all_to_all x2, blocking collectives, all_sum(): held = jnp.sum(lax.all_to_all(copies, axes, 0, 0, tiled=True), axis=0)  29.4 us
    ppermute x5, starting transfers between devices, send(): return lax.ppermute(what, AXES, swapped(count_x, count_y, pair, flip))  22.1 us
    pallas_call x1, Pallas kernels, per_device(): pl.pallas_call(functools.partial(lower_kernel, geom), out_shape=(jax.Shap...  7.09 us
    pallas_call x1, Pallas kernels, per_device(): pl.pallas_call(functools.partial(mix_kernel, geom, total_size), out_shape...  4.88 us
    ppermute x1, starting transfers between devices, all_sum(): held = mine + lax.ppermute(other, 'gx_3', swap)  3.61 us
    pallas_call x1, Pallas kernels, per_device(): pl.pallas_call(functools.partial(pack_kernel, geom), out_shape=(jax.Shape...  2.98 us
    pallas_call x1, Pallas kernels, per_device(): pl.pallas_call(functools.partial(upper_kernel, geom), out_shape=jax.Shape...  2.68 us
    ppermute x1, starting transfers between devices, all_sum(): return (held, lax.ppermute(held, 'gx_3', swap))  2.52 us
  transfers between devices with their start and end apart: 7, of which 3 were waited for; matrix products, arithmetic and copies ran while one was open for 0% of the time, Pallas kernels for 5%

commit v1 on v0

--- a/solution.py
+++ b/solution.py
@@ -9,6 +9,7 @@
 from jax.sharding import PartitionSpec as P
 
 TILE = 4
+HALF = TILE // 2
 LANES = 128
 GX = ("gx_0", "gx_1", "gx_2", "gx_3")
 AXES = GX + ("gy",)
@@ -55,7 +56,7 @@
 
 
 def pack_kernel(
-    geom, part_hbm, back_hbm, tile_hbm, mask_hbm, value_hbm, var_hbm, main_ref, edge_ref, table_ref,
+    geom, part_hbm, back_hbm, tile_hbm, mask_hbm, value_hbm, var_hbm, near_ref, far_ref, edge_ref, table_ref,
     part_ref, back_ref, tile_ref, mask_ref, value_ref, var_ref, sems,
 ):
     count, layers, rows, cols = geom
@@ -73,8 +74,8 @@
     for copy in copies[:5]:
         copy.wait()
     tile = tile_ref[...].astype(f32)
-    top = layers * rows * count + count // tiles
-    main_ref[top : top + 8, :] = jnp.zeros((8, cols), f32)
+    top = layers * HALF * count + count // tiles
+    far_ref[top : top + 8, :] = jnp.zeros((8, cols), f32)
     facts = []
     for r in range(rows):
         source = r + flip * (rows - 1 - 2 * r)
@@ -82,7 +83,7 @@
         facts += masks
         table_ref[r * cols : (r + 1) * cols, :] = own_table(masks, tile, cols)
     for k, fact in enumerate(facts + [tile, var_ref[...]]):
-        main_ref[top + k // tiles : top + k // tiles + 1, (k % tiles) * LANES : (k % tiles + 1) * LANES] = fact
+        far_ref[top + k // tiles : top + k // tiles + 1, (k % tiles) * LANES : (k % tiles + 1) * LANES] = fact
     copies[5].wait()
     edge = jnp.zeros((count, LANES), f32)
     seen = jnp.zeros((count, LANES), f32)
@@ -91,12 +92,13 @@
             source = r + flip * (rows - 1 - 2 * r)
             base = (l * rows + r) * 2 * TILE + TILE
             back = stored_row(back_ref, l, r, rows, flip)
+            half_ref, start = (near_ref, far_ref)[r // HALF], (l * HALF + r % HALF) * count
             state = []
             for ct in range(tiles):
                 cell = part_ref[pl.ds((l * tiles + ct) * rows + source, count, stride=per), :]
                 state.append(cell)
                 dev = cell - back[:, ct * LANES : (ct + 1) * LANES]
-                main_ref[(l * rows + r) * count : (l * rows + r + 1) * count, ct * LANES : (ct + 1) * LANES] = dev
+                half_ref[start : start + count, ct * LANES : (ct + 1) * LANES] = dev
                 if ct == 0:
                     rolled = pltpu.roll(dev, base, axis=1)
                     edge = jnp.where((lane >= base) & (lane < base + TILE), rolled, edge)
@@ -114,16 +116,16 @@
             rolled = pltpu.roll(dot_exact(pull, table, ((1,), (1,))), base, axis=1)
             edge = jnp.where((lane >= low) & (lane < low + TILE), rolled, edge)
     edge_ref[...] = edge
-    top = layers * rows * count
+    top = layers * HALF * count
     part = count // tiles
     for ct in range(tiles):
-        main_ref[top : top + part, ct * LANES : (ct + 1) * LANES] = pull[ct * part : (ct + 1) * part]
+        far_ref[top : top + part, ct * LANES : (ct + 1) * LANES] = pull[ct * part : (ct + 1) * part]
 
 
 def fetch_main(geom, ref):
-    count, layers, rows, cols = geom
+    count, layers, _, cols = geom
     tiles = cols // LANES
-    top = layers * rows * count + count // tiles
+    top = layers * HALF * count + count // tiles
 
     def fetch(k):
         return ref[top + k // tiles : top + k // tiles + 1, (k % tiles) * LANES : (k % tiles + 1) * LANES]
@@ -132,8 +134,8 @@
 
 
 def pull_main(geom, ref):
-    count, layers, rows, cols = geom
-    top, tiles = layers * rows * count, cols // LANES
+    count, layers, _, cols = geom
+    top, tiles = layers * HALF * count, cols // LANES
     part = count // tiles
     return jnp.concatenate([ref[top : top + part, ct * LANES : (ct + 1) * LANES] for ct in range(tiles)], axis=0)
 
@@ -161,17 +163,25 @@
     return total
 
 
-def local_kernel(geom, own_ref, table_ref, spread_ref, square_ref, *dev_refs):
+def slab_row(halves, count, l, r):
+    start = (l * HALF + r % HALF) * count
+    return halves[r // HALF][start : start + count, :]
+
+
+def local_kernel(geom, near_ref, far_ref, table_ref, spread_ref, square_ref, *dev_refs):
     count, layers, rows, cols = geom
-    pull = pull_main(geom, own_ref)
+    pull = pull_main(geom, far_ref)
     for r in range(rows):
         spread_ref[r * count : (r + 1) * count, :] = dot_exact(
             pull, table_ref[r * cols : (r + 1) * cols, :], ((1,), (1,))
         )
-    for k in range(layers * rows):
-        for ref, piece in zip(dev_refs, pieces(own_ref[k * count : (k + 1) * count, :])):
-            ref[:, k * cols : (k + 1) * cols] = piece
-    square_ref[...] = gram_self(dev_refs)
+    for l in range(layers):
+        for r in range(rows):
+            k = l * HALF + r % HALF
+            half = dev_refs[3 * (r // HALF) : 3 * (r // HALF) + 3]
+            for ref, piece in zip(half, pieces(slab_row((near_ref, far_ref), count, l, r))):
+                ref[:, k * cols : (k + 1) * cols] = piece
+    square_ref[...] = gram_self(dev_refs[:3]) + gram_self(dev_refs[3:])
 
 
 def edge_tile(side_ref, slot):
@@ -195,26 +205,25 @@
             store(l, r, mine, (-prior_weight / 16.0) * (curved + 16.0 * couple_weight * (mine - field(1 - l, r))))
 
 
-def gradient_rows(geom, which, own_ref, far_ref, side_ref, side_far_ref, far_row, spread_ref, out_ref):
+def gradient_rows(geom, which, own, other, side_ref, side_other_ref, other_row, spread_ref, out_ref):
     count, layers, rows, cols = geom
-    far_pull, far_fetch = pull_main(geom, far_ref), fetch_main(geom, far_ref)
 
     def row_of(r):
-        return (own_ref, side_ref, r) if 0 <= r < rows else (far_ref, side_far_ref, far_row(r))
+        return (own, side_ref, r) if 0 <= r < rows else (other, side_other_ref, other_row(r))
 
     def field(l, r):
-        ref, side, rr = row_of(r)
-        start = (l * rows + rr) * count
-        return jnp.concatenate([ref[start : start + count, :], edge_tile(side, l * rows + rr)], axis=1)
+        halves, side, rr = row_of(r)
+        return jnp.concatenate([slab_row(halves, count, l, rr), edge_tile(side, l * rows + rr)], axis=1)
 
     def put(l, r, mine, out):
         if l == 0:
-            _, side, rr = row_of(r)
+            halves, side, rr = row_of(r)
             if 0 <= r < rows:
                 inner = spread_ref[r * count : (r + 1) * count, :]
             else:
-                table = own_table(masks_of(far_fetch, rr), far_fetch(rows * TILE), cols)
-                inner = dot_exact(far_pull, table, ((1,), (1,)))
+                fetch = fetch_main(geom, halves[1])
+                table = own_table(masks_of(fetch, rr), fetch(rows * TILE), cols)
+                inner = dot_exact(pull_main(geom, halves[1]), table, ((1,), (1,)))
             out = out + jnp.concatenate([inner, edge_tile(side, layers * rows + rr)], axis=1)
         start = (l * len(which) + r - which[0]) * count
         out_ref[start : start + count, :] = out
@@ -222,46 +231,83 @@
     prior_rows(layers, which, field, put)
 
 
-def upper_kernel(geom, own_ref, high_ref, side_ref, side_high_ref, spread_ref, up_ref):
+def upper_kernel(
+    geom, near_ref, far_ref, high_near_ref, high_far_ref, side_ref, side_high_ref, spread_ref, up_ref
+):
     rows = geom[2]
     which = tuple(range(rows - 2, rows + 2))
-    far_row = lambda r: 2 * rows - 1 - r
-    gradient_rows(geom, which, own_ref, high_ref, side_ref, side_high_ref, far_row, spread_ref, up_ref)
-
-
-def lower_kernel(
-    geom, own_ref, low_ref, side_ref, side_low_ref, spread_ref, up_ref, table_ref, square_ref,
-    dev_hi, dev_mid, dev_lo, grad_ref, hess_ref, mine_ref, other_ref, hi_ref, mid_ref, lo_ref, down, full,
-):
-    count, layers, rows, cols = geom
-    far_row = lambda r: -1 - r
-    gradient_rows(geom, (-2, -1, 0, 1), own_ref, low_ref, side_ref, side_low_ref, far_row, spread_ref, down)
-
-    def whole(l, r):
-        ref, slot = (down, r + 2) if r < 2 else (up_ref, r - rows + 2)
-        start = (l * 4 + slot) * count
-        return ref[start : start + count, :]
-
-    table = lambda r: table_ref[r * cols : (r + 1) * cols, :]
-    seen = sum(dot_exact(whole(0, r)[:, 0:cols], table(r), ((1,), (0,))) for r in range(rows))
-    pull = -0.0625 * seen / fetch_main(geom, own_ref)(rows * TILE + 1)
-    parts = (hi_ref, mid_ref, lo_ref)
+    own, other = (near_ref, far_ref), (high_near_ref, high_far_ref)
+    other_row = lambda r: 2 * rows - 1 - r
+    gradient_rows(geom, which, own, other, side_ref, side_high_ref, other_row, spread_ref, up_ref)
+
+
+def gradient_at(count, l, r, down_ref, mid_ref, up_ref):
+    if r < 0:
+        ref, start = down_ref, (l * 2 + r + 2) * count
+    elif r < 2:
+        ref, start = mid_ref, (l * 2 + r) * count
+    else:
+        ref, start = up_ref, (l * 4 + r - 2) * count
+    return ref[start : start + count, :]
+
+
+def linear_rows(geom, which, field, extra, hess_ref, parts):
+    count, layers, _, cols = geom
 
     def put(l, r, mine, out):
         out = out[:, 0:cols]
         if l == 0:
-            out = out + dot_exact(pull, table(r), ((1,), (1,)))
-        k = l * rows + r
-        grad_ref[k * count : (k + 1) * count, :] = mine[:, 0:cols]
+            out = out + extra(r)
+        k = l * HALF + r % HALF
         hess_ref[k * count : (k + 1) * count, :] = out
         span = slice(k * cols, (k + 1) * cols)
         for ref, grad, hess in zip(parts, pieces(mine[:, 0:cols]), pieces(out)):
             ref[0:count, span] = grad
             ref[count:, span] = hess
 
-    prior_rows(layers, tuple(range(rows)), whole, put)
-    with_dev = gram_cross(parts, (dev_hi, dev_mid, dev_lo))
-    total = gram_self(parts)
+    prior_rows(layers, which, field, put)
+
+
+def middle_kernel(
+    geom, near_ref, far_ref, low_near_ref, side_ref, side_low_ref, spread_ref, up_ref, table_ref,
+    dev_hi, dev_mid, dev_lo, mid_ref, grad_near_ref, grad_far_ref, hess_ref, spread_two_ref, with_dev_ref, self_ref,
+    *parts,
+):
+    count, layers, rows, cols = geom
+    own = (near_ref, far_ref)
+    other_row = lambda r: -1 - r
+    gradient_rows(geom, (0, 1), own, (low_near_ref, None), side_ref, side_low_ref, other_row, spread_ref, mid_ref)
+    field = lambda l, r: gradient_at(count, l, r, None, mid_ref, up_ref)
+    for l in range(layers):
+        for r in range(rows):
+            start = (l * HALF + r % HALF) * count
+            (grad_near_ref, grad_far_ref)[r // HALF][start : start + count, :] = field(l, r)[:, 0:cols]
+    table = lambda r: table_ref[r * cols : (r + 1) * cols, :]
+    seen = sum(dot_exact(field(0, r)[:, 0:cols], table(r), ((1,), (0,))) for r in range(rows))
+    pull = -0.0625 * seen / fetch_main(geom, far_ref)(rows * TILE + 1)
+    for r in range(HALF):
+        spread_two_ref[r * count : (r + 1) * count, :] = dot_exact(pull, table(r), ((1,), (1,)))
+    extra = lambda r: dot_exact(pull, table(r), ((1,), (1,)))
+    linear_rows(geom, (2, 3), field, extra, hess_ref, parts)
+    with_dev_ref[...] = gram_cross(parts, (dev_hi, dev_mid, dev_lo))
+    self_ref[...] = gram_self(parts)
+
+
+def lower_kernel(
+    geom, near_ref, far_ref, low_near_ref, low_far_ref, side_ref, side_low_ref, mid_ref, up_ref, spread_two_ref,
+    square_ref, with_dev_ref, self_ref, dev_hi, dev_mid, dev_lo, hess_ref, mine_ref, other_ref,
+    hi_ref, mid_part_ref, lo_ref, down, full,
+):
+    count, _, _, _ = geom
+    own, other = (near_ref, far_ref), (low_near_ref, low_far_ref)
+    other_row = lambda r: -1 - r
+    gradient_rows(geom, (-2, -1), own, other, side_ref, side_low_ref, other_row, None, down)
+    field = lambda l, r: gradient_at(count, l, r, down, mid_ref, up_ref)
+    extra = lambda r: spread_two_ref[r * count : (r + 1) * count, :]
+    parts = (hi_ref, mid_part_ref, lo_ref)
+    linear_rows(geom, (0, 1), field, extra, hess_ref, parts)
+    with_dev = gram_cross(parts, (dev_hi, dev_mid, dev_lo)) + with_dev_ref[...]
+    total = gram_self(parts) + self_ref[...]
     c = count
     row = lax.broadcasted_iota(jnp.int32, (c, c), 0)
     col = lax.broadcasted_iota(jnp.int32, (c, c), 1)
@@ -285,7 +331,8 @@
 
 
 def mix_kernel(
-    geom, total_size, mine_ref, other_ref, own_ref, grad_ref, hess_ref, back_ref, out_ref, full
+    geom, total_size, mine_ref, other_ref, near_ref, far_ref, grad_near_ref, grad_far_ref, hess_near_ref, hess_far_ref,
+    back_ref, out_ref, full,
 ):
     count, layers, rows, cols = geom
     tiles = cols // LANES
@@ -349,11 +396,11 @@
     lefts = (jnp.concatenate(mix, axis=0), jnp.concatenate(mix[:2], axis=0), mix[0])
     for l in range(layers):
         for r in range(rows):
-            k = l * rows + r
-            span = slice(k * c, (k + 1) * c)
             source = r + flip * (rows - 1 - 2 * r)
-            own = own_ref[span, :]
-            stack = pieces(jnp.concatenate([own, grad_ref[span, :], hess_ref[span, :]], axis=0))
+            own = slab_row((near_ref, far_ref), c, l, r)
+            grad = slab_row((grad_near_ref, grad_far_ref), c, l, r)
+            hess = slab_row((hess_near_ref, hess_far_ref), c, l, r)
+            stack = pieces(jnp.concatenate([own, grad, hess], axis=0))
             parts = [
                 lax.dot_general(a, b, (((1,), (0,)), ((), ())), preferred_element_type=f32)
                 for a, b in zip(lefts, stack)
@@ -395,15 +442,18 @@
     total_size = float(layers * rows * cols * count_x * count_y)
     flat = particles.reshape(count, layers, rows, tiles, LANES).transpose(0, 1, 3, 2, 4)
     flat = flat.reshape(count * layers * rows * tiles, LANES)
-    block = layers * rows * count
+    half = layers * HALF * count
+    wide = cols + LANES
     params = pltpu.CompilerParams(vmem_limit_bytes=24 * 1024 * 1024)
+    shape = jax.ShapeDtypeStruct
     inputs = (flat, background, obs_tile, obs_mask, obs_value, obs_var)
-    main, edge, table = pl.pallas_call(
+    near, far, edge, table = pl.pallas_call(
         functools.partial(pack_kernel, geom),
         out_shape=(
-            jax.ShapeDtypeStruct((block + count // tiles + 8, cols), f32),
-            jax.ShapeDtypeStruct((count, LANES), f32),
-            jax.ShapeDtypeStruct((rows * cols, LANES), bf16),
+            shape((half, cols), f32),
+            shape((half + count // tiles + 8, cols), f32),
+            shape((count, LANES), f32),
+            shape((rows * cols, LANES), bf16),
         ),
         in_specs=[pl.BlockSpec(memory_space=pltpu.HBM)] * len(inputs),
         scratch_shapes=[pltpu.VMEM(a.shape, a.dtype) for a in inputs] + [pltpu.SemaphoreType.DMA((len(inputs),))],
@@ -415,45 +465,57 @@
         return lax.ppermute(what, AXES, swapped(count_x, count_y, pair, flip))
 
     side = send(edge, None, True)
-    low = send(main, 1, False)
-    high = send(main, 0, False)
+    low_near = send(near, 1, False)
     side_low = send(side, 1, False)
+    low_far = send(far, 1, False)
+    high_near = send(near, 0, False)
+    high_far = send(far, 0, False)
     side_high = send(side, 0, False)
-    half = jax.ShapeDtypeStruct((count, block // count * cols), bf16)
+    piece = shape((count, layers * HALF * cols), bf16)
     spread, square, *dev = pl.pallas_call(
         functools.partial(local_kernel, geom),
-        out_shape=(
-            jax.ShapeDtypeStruct((rows * count, cols), f32),
-            jax.ShapeDtypeStruct((count, count), f32),
-        )
-        + (half,) * 3,
+        out_shape=(shape((rows * count, cols), f32), shape((count, count), f32)) + (piece,) * 6,
         compiler_params=params,
         name="local",
-    )(main, table)
+    )(near, far, table)
     up = pl.pallas_call(
         functools.partial(upper_kernel, geom),
-        out_shape=jax.ShapeDtypeStruct((layers * 4 * count, cols + LANES), f32),
+        out_shape=shape((layers * 4 * count, wide), f32),
         compiler_params=params,
         name="upper",
-    )(main, high, side, side_high, spread)
+    )(near, far, high_near, high_far, side, side_high, spread)
+    parts = [pltpu.VMEM((2 * count, piece.shape[1]), bf16)] * 3
+    mid, grad_near, grad_far, hess_far, spread_two, with_dev, total = pl.pallas_call(
+        functools.partial(middle_kernel, geom),
+        out_shape=(
+            shape((half, wide), f32),
+            shape((half, cols), f32),
+            shape((half, cols), f32),
+            shape((half, cols), f32),
+            shape((HALF * count, cols), f32),
+            shape((2 * count, count), f32),
+            shape((2 * count, 2 * count), f32),
+        ),
+        scratch_shapes=parts,
+        compiler_params=params,
+        name="middle",
+    )(near, far, low_near, side, side_low, spread, up, table, *dev[3:])
     full = pltpu.VMEM((7 * count // 4, LANES), f32)
-    grad, hess, mine, other = pl.pallas_call(
+    hess_near, mine, other = pl.pallas_call(
         functools.partial(lower_kernel, geom),
-        out_shape=(jax.ShapeDtypeStruct((block, cols), f32),) * 2
-        + (jax.ShapeDtypeStruct((7 * count // 8, LANES), f32),) * 2,
-        scratch_shapes=[pltpu.VMEM((2 * count, half.shape[1]), bf16)] * 3
-        + [pltpu.VMEM((layers * 4 * count, cols + LANES), f32), full],
+        out_shape=(shape((half, cols), f32),) + (shape((7 * count // 8, LANES), f32),) * 2,
+        scratch_shapes=parts + [pltpu.VMEM((half, wide), f32), full],
         compiler_params=params,
         name="lower",
-    )(main, low, side, side_low, spread, up, table, square, *dev)
+    )(near, far, low_near, low_far, side, side_low, mid, up, spread_two, square, with_dev, total, *dev[:3])
     mine, other = all_sum(mine, other)
     out = pl.pallas_call(
         functools.partial(mix_kernel, geom, total_size),
-        out_shape=jax.ShapeDtypeStruct(flat.shape, f32),
+        out_shape=shape(flat.shape, f32),
         scratch_shapes=[full],
         compiler_params=params,
         name="mix",
-    )(mine, other, main, grad, hess, background)
+    )(mine, other, near, far, grad_near, grad_far, hess_near, hess_far, background)
     out = out.reshape(count, layers, tiles, rows, LANES).transpose(0, 1, 3, 2, 4)
     return out.reshape(geom)
 

time: 81.2 us -> 83.3 us (1.026)
  waiting for transfers between devices: 3.16 us -> 12.6 us
  starting transfers between devices: 28.2 us -> 22.5 us
  blocking collectives: 29.4 us -> 26.8 us
  Pallas kernels: 18.9 us -> 19.9 us
    ppermute x5 -> x7, waiting for transfers between devices: 1.45 us -> 10.9 us  [send(): return lax.ppermute(what, AXES, swapped(count_x, count_y, pair, flip))]
    ppermute x5 -> x7, starting transfers between devices: 22.1 us -> 13.9 us  [send(): return lax.ppermute(what, AXES, swapped(count_x, count_y, pair, flip))]
    all_to_all x2, blocking collectives: 29.4 us -> 26.8 us  [all_sum(): held = jnp.sum(lax.all_to_all(copies, axes, 0, 0, tiled=True), axis=0)]
    ppermute x1, starting transfers between devices: 3.61 us -> 6.12 us  [all_sum(): held = mine + lax.ppermute(other, 'gx_3', swap)]
    pallas_call x4 -> x5, Pallas kernels: 14.1 us -> 15 us  [the longest x1 4.05 us: per_device(): pl.pallas_call(functools.partial(middle_kernel, geom), out_shape=(shape((...]
  transfers between devices with their start and end apart: 7 -> 9, of which waited for: 3 -> 4; matrix products, arithmetic and copies ran while one was open for 0% -> 0% of each run, Pallas kernels for 5% -> 10%
where the time goes in v1:
time: 83.3 us; the launch traced here: 83 us
  blocking collectives  26.8 us (32%)
  starting transfers between devices  22.5 us (27%)
  Pallas kernels  19.9 us (24%)
  waiting for transfers between devices  12.6 us (15%)
  other arithmetic  1.07 us (1%)
    all_to_all x2, blocking collectives, all_sum(): held = jnp.sum(lax.all_to_all(copies, axes, 0, 0, tiled=True), axis=0)  26.8 us
    ppermute x7, starting transfers between devices, send(): return lax.ppermute(what, AXES, swapped(count_x, count_y, pair, flip))  13.9 us
    ppermute x7, waiting for transfers between devices, send(): return lax.ppermute(what, AXES, swapped(count_x, count_y, pair, flip))  10.9 us
    ppermute x1, starting transfers between devices, all_sum(): held = mine + lax.ppermute(other, 'gx_3', swap)  6.12 us
    pallas_call x1, Pallas kernels, per_device(): pl.pallas_call(functools.partial(mix_kernel, geom, total_size), out_shape...  4.88 us
    pallas_call x1, Pallas kernels, per_device(): pl.pallas_call(functools.partial(middle_kernel, geom), out_shape=(shape((...  4.05 us
    pallas_call x1, Pallas kernels, per_device(): pl.pallas_call(functools.partial(lower_kernel, geom), out_shape=(shape((h...  3.98 us
    pallas_call x1, Pallas kernels, per_device(): pl.pallas_call(functools.partial(pack_kernel, geom), out_shape=(shape((ha...  2.98 us
  transfers between devices with their start and end apart: 9, of which 4 were waited for; matrix products, arithmetic and copies ran while one was open for 0% of the time, Pallas kernels for 10%

profile of v1, /device:TPU:1, one launch (start us, length us, event | category | flops | bytes accessed | tf_op | source)
XLA Modules:
  0.0 83.0 jit_solution(216568658544641434)
XLA Ops:
  0.0 3.0 %pack.1 = (f32[256,512]{1,0:T(8,128)S(1)}, f32[280,512]{1,0:T(8,128)S(1)}, f32[64,128]{1,0:T(8,128)S(1)}, bf16[2048,128]{1,0:T(8,128)(2,1)S(1)}) custom-call(f32[2048,128]{1,0:T(8,128)} %bitcast.10, f32[2,4,512]{2,1,0:T(4,128)} %back_ref.1, s32[1,128]{1,0:T(1,128)} %tile_hbm.1, s32[16,1,128]{2,1,0:T(1,128)} %mask_hbm.1, f32[1,128]{1,0:T(1,128)} %value_hbm.1, ...), custom_call_target="tpu_custom_call" | custom-call | tf_op jit(solution)/shard_map/pack/pallas_call | solution.py:450
  3.0 3.3 %collective-permute-start.5 = (f32[280,512]{1,0:T(8,128)S(1)}, f32[280,512]{1,0:T(8,128)S(1)}, u32[]{:S(2)}, u32[]{:S(2)}) collective-permute-start(f32[280,512]{1,0:T(8,128)S(1)} %get-tuple-element.28.far_ref), channel_id=1, source_target_pairs={{0,2},{1,3},{2,0},{3,1},{4,6},{5,7},{6,4},{7,5},{8,10},{9,11},{10,... | collective-permute-start | bytes 1720328 | tf_op jit(solution)/shard_map/ppermute | solution.py:465
  6.3 0.0 collective-permute-start.1
  6.3 7.5 %collective-permute-start.4 = (f32[256,512]{1,0:T(8,128)S(1)}, f32[256,512]{1,0:T(8,128)S(1)}, u32[]{:S(2)}, u32[]{:S(2)}) collective-permute-start(f32[256,512]{1,0:T(8,128)S(1)} %get-tuple-element.27.near_ref), channel_id=1, source_target_pairs={{0,2},{1,3},{2,0},{3,1},{4,6},{5,7},{6,4},{7,5},{8,10},{9,11},{10,... | collective-permute-start | bytes 1572872 | tf_op jit(solution)/shard_map/ppermute | solution.py:465
  13.7 0.0 collective-permute-start
  13.8 2.6 %collective-permute-start.2 = (f32[64,128]{1,0:T(8,128)S(1)}, f32[64,128]{1,0:T(8,128)S(1)}, u32[]{:S(2)}, u32[]{:S(2)}) collective-permute-start(f32[64,128]{1,0:T(8,128)S(1)} %get-tuple-element.29), channel_id=1, source_target_pairs={{0,1},{1,0},{2,3},{3,2},{4,5},{5,4},{6,7},{7,6},{8,9},{9,8},{10,11... | collective-permute-start | bytes 98312 | tf_op jit(solution)/shard_map/ppermute | solution.py:465
  16.4 10.0 %collective-permute-done.2.side_ref = f32[64,128]{1,0:T(8,128)S(1)} collective-permute-done((f32[64,128]{1,0:T(8,128)S(1)}, f32[64,128]{1,0:T(8,128)S(1)}, u32[]{:S(2)}, u32[]{:S(2)}) %collective-permute-start.2) | collective-permute-done | bytes 32800 | tf_op jit(solution)/shard_map/ppermute | solution.py:465
  26.4 0.5 collective-permute-start.6
  26.9 0.9 %collective-permute-done.6.side_high_ref = f32[64,128]{1,0:T(8,128)S(1)} collective-permute-done((f32[64,128]{1,0:T(8,128)S(1)}, f32[64,128]{1,0:T(8,128)S(1)}, u32[]{:S(2)}, u32[]{:S(2)}) %collective-permute-start.6) | collective-permute-done | bytes 32800 | tf_op jit(solution)/shard_map/ppermute | solution.py:465
  27.7 0.0 collective-permute-start.3
  27.7 1.3 %local.1 = (f32[256,512]{1,0:T(8,128)S(1)}, f32[64,64]{1,0:T(8,128)S(1)}, bf16[64,2048]{1,0:T(8,128)(2,1)S(1)}, bf16[64,2048]{1,0:T(8,128)(2,1)S(1)}, bf16[64,20...) custom-call(f32[256,512]{1,0:T(8,128)S(1)} %get-tuple-element.27.nea, ...), custom_call_target="tpu_custom_call" | custom-call | tf_op jit(solution)/shard_map/local/pallas_call | solution.py:475
  29.1 0.0 collective-permute-done.4.high_near_ref
  29.1 0.0 collective-permute-done.5.high_far_ref
  29.1 2.7 %upper.1.up_ref = f32[512,640]{1,0:T(8,128)S(1)} custom-call(f32[256,512]{1,0:T(8,128)S(1)} %get-tuple-element.27.near_ref, f32[280,512]{1,0:T(8,128)S(1)} %get-tuple-element.28.far_ref, f32[256,512]{1,0:T(8,128)S(1)} %collective-permute-done.4.high_near_ref, f32[280,512]{1,0:T(8,128)S(1)} %collective-permute-done.5.high_far_ref, ...), custom_call_target="tpu_custom_call" | custom-call | tf_op jit(solution)/shard_map/upper/pallas_call | solution.py:481
  31.8 0.0 collective-permute-done.3.side_low_ref
  31.8 0.0 collective-permute-done.low_near_ref
  31.8 4.1 %middle.1 = (f32[256,640]{1,0:T(8,128)S(1)}, f32[256,512]{1,0:T(8,128)S(1)}, f32[256,512]{1,0:T(8,128)S(1)}, f32[256,512]{1,0:T(8,128)S(1)}, f32[128,512]{1,0:T(...) custom-call(f32[256,512]{1,0:T(8,128)S(1)} %get-tuple-element.27.near_ref, ...), custom_call_target="tpu_custom_call" | custom-call | tf_op jit(solution)/shard_map/middle/pallas_call | solution.py:488
  35.9 0.0 collective-permute-done.1.low_far_ref
  35.9 4.0 %lower.1 = (f32[256,512]{1,0:T(8,128)S(1)}, f32[56,128]{1,0:T(8,128)S(1)}, f32[56,128]{1,0:T(8,128)S(1)}) custom-call(f32[256,512]{1,0:T(8,128)S(1)} %get-tuple-element.27.near_ref, f32[280,512]{1,0:T(8,128)S(1)} %get-tuple-element.28.far_ref, f32[256,512]{1,0:T(8,128)S(1)} %collective-permute-done.low_near_ref, ...), custom_call_target="tpu_custom_call" | custom-call | tf_op jit(solution)/shard_map/lower/pallas_call | solution.py:504
  39.9 6.1 %collective-permute-start.7 = (f32[56,128]{1,0:T(8,128)S(1)}, f32[56,128]{1,0:T(8,128)S(1)}, u32[]{:S(2)}, u32[]{:S(2)}) collective-permute-start(f32[56,128]{1,0:T(8,128)S(1)} %get-tuple-element.44), channel_id=1, source_target_pairs={{0,2},{2,0},{1,3},{3,1},{4,6},{6,4},{5,7},{7,5},{8,10},{10,8},{9,1... | collective-permute-start | bytes 86024 | tf_op jit(solution)/shard_map/ppermute | solution.py:417
  46.0 0.9 %collective-permute-done.7 = f32[56,128]{1,0:T(8,128)S(1)} collective-permute-done((f32[56,128]{1,0:T(8,128)S(1)}, f32[56,128]{1,0:T(8,128)S(1)}, u32[]{:S(2)}, u32[]{:S(2)}) %collective-permute-start.7) | collective-permute-done | bytes 28704 | tf_op jit(solution)/shard_map/ppermute | solution.py:417
  46.9 0.0 copy-start
  46.9 14.0 %all_to_all.10 = f32[8,56,128]{2,1,0:T(8,128)S(1)} all-to-all(f32[8,56,128]{2,1,0:T(8,128)S(1)} %broadcast_in_dim.6), channel_id=1, replica_groups=mesh['gx_0'=4,'gx_1'=2,'gx_2'=8,'gx_3'=2,'gy'=2] {'gx_2'}, dimensions={0} | all-to-all | bytes 458752 | tf_op jit(solution)/shard_map/all_to_all | solution.py:423
  60.9 12.9 %all_to_all.11 = f32[16,56,128]{2,1,0:T(8,128)} all-to-all(f32[16,56,128]{2,1,0:T(8,128)S(1)} %broadcast_in_dim.7), channel_id=1, replica_groups=mesh['gx_0'=4,'gx_1'=2,'gx_2'=8,'gx_3'=2,'gy'=2] {'gx_0','gx_1','gy'}, dimensions={0} | all-to-all | bytes 917504 | tf_op jit(solution)/shard_map/all_to_all | solution.py:423
  73.7 1.1 %reduce_sum.19.mine_ref = f32[56,128]{1,0:T(8,128)S(1)} reduce(f32[16,56,128]{2,1,0:T(8,128)} %all_to_all.11, f32[]{:T(128)} %constant.0.clone.1), dimensions={0}, to_apply=%region_1.0 | reduce | flops 107520 | bytes 487428 | tf_op jit(solution)/shard_map/reduce_sum | solution.py:423
  74.8 2.5 %collective-permute-start.8 = (f32[56,128]{1,0:T(8,128)S(1)}, f32[56,128]{1,0:T(8,128)S(1)}, u32[]{:S(2)}, u32[]{:S(2)}) collective-permute-start(f32[56,128]{1,0:T(8,128)S(1)} %reduce_sum.19.mine_ref), channel_id=1, source_target_pairs={{0,2},{2,0},{1,3},{3,1},{4,6},{6,4},{5,7},{7,5},{8,10},{10,8},{9,1... | collective-permute-start | bytes 86024 | tf_op jit(solution)/shard_map/ppermute | solution.py:424
  77.3 0.9 %collective-permute-done.8.other_ref = f32[56,128]{1,0:T(8,128)S(1)} collective-permute-done((f32[56,128]{1,0:T(8,128)S(1)}, f32[56,128]{1,0:T(8,128)S(1)}, u32[]{:S(2)}, u32[]{:S(2)}) %collective-permute-start.8) | collective-permute-done | bytes 28704 | tf_op jit(solution)/shard_map/ppermute | solution.py:424
  78.2 0.0 copy-done
  78.2 4.9 %mix.1 = f32[2048,128]{1,0:T(8,128)} custom-call(f32[56,128]{1,0:T(8,128)S(1)} %reduce_sum.19.mine_ref, f32[56,128]{1,0:T(8,128)S(1)} %collective-permute-done.8.other_ref, f32[256,512]{1,0:T(8,128)S(1)} %get-tuple-element.27.near_ref, f32[280,512]{1,0:T(8,128)S(1)} %get-tuple-element.28.far_ref, f32[256,512]{1,0:T(8,128)S(1)} %get-tuple-element.45.grad_near_ref, ...), custom_call_target="tpu_custom_call" | custom-call | tf_op jit(solution)/shard_map/mix/pallas_call | solution.py:512
  (4 shorter events, 0.1 us)
Async XLA Ops:
  3.0 26.1 %collective-permute-start.5 = (f32[280,512]{1,0:T(8,128)S(1)}, f32[280,512]{1,0:T(8,128)S(1)}, u32[]{:S(2)}, u32[]{:S(2)}) collective-permute-start(f32[280,512]{1,0:T(8,128)S(1)} %get-tuple-element.28.far_ref), channel_id=1, source_target_pairs={{0,2},{1,3},{2,0},{3,1},{4,6},{5,7},{6,4},{7,5},{8,10},{9,11},{10,... | collective-permute-start | bytes 1720328 | tf_op jit(solution)/shard_map/ppermute | solution.py:465
  6.3 29.6 %collective-permute-start.1 = (f32[280,512]{1,0:T(8,128)S(1)}, f32[280,512]{1,0:T(8,128)S(1)}, u32[]{:S(2)}, u32[]{:S(2)}) collective-permute-start(f32[280,512]{1,0:T(8,128)S(1)} %get-tuple-element.28.far_ref), channel_id=1, source_target_pairs={{0,254},{1,255},{2,4},{3,5},{4,2},{5,3},{6,8},{7,9},{8,6},{9,7},{1... | collective-permute-start | bytes 1720328 | tf_op jit(solution)/shard_map/ppermute | solution.py:465
  6.3 22.8 %collective-permute-start.4 = (f32[256,512]{1,0:T(8,128)S(1)}, f32[256,512]{1,0:T(8,128)S(1)}, u32[]{:S(2)}, u32[]{:S(2)}) collective-permute-start(f32[256,512]{1,0:T(8,128)S(1)} %get-tuple-element.27.near_ref), channel_id=1, source_target_pairs={{0,2},{1,3},{2,0},{3,1},{4,6},{5,7},{6,4},{7,5},{8,10},{9,11},{10,... | collective-permute-start | bytes 1572872 | tf_op jit(solution)/shard_map/ppermute | solution.py:465
  13.7 18.0 %collective-permute-start = (f32[256,512]{1,0:T(8,128)S(1)}, f32[256,512]{1,0:T(8,128)S(1)}, u32[]{:S(2)}, u32[]{:S(2)}) collective-permute-start(f32[256,512]{1,0:T(8,128)S(1)} %get-tuple-element.27.near_ref), channel_id=1, source_target_pairs={{0,254},{1,255},{2,4},{3,5},{4,2},{5,3},{6,8},{7,9},{8,6},{9,7},{1... | collective-permute-start | bytes 1572872 | tf_op jit(solution)/shard_map/ppermute | solution.py:465
  13.8 12.6 %collective-permute-start.2 = (f32[64,128]{1,0:T(8,128)S(1)}, f32[64,128]{1,0:T(8,128)S(1)}, u32[]{:S(2)}, u32[]{:S(2)}) collective-permute-start(f32[64,128]{1,0:T(8,128)S(1)} %get-tuple-element.29), channel_id=1, source_target_pairs={{0,1},{1,0},{2,3},{3,2},{4,5},{5,4},{6,7},{7,6},{8,9},{9,8},{10,11... | collective-permute-start | bytes 98312 | tf_op jit(solution)/shard_map/ppermute | solution.py:465
  26.4 1.4 %collective-permute-start.6 = (f32[64,128]{1,0:T(8,128)S(1)}, f32[64,128]{1,0:T(8,128)S(1)}, u32[]{:S(2)}, u32[]{:S(2)}) collective-permute-start(f32[64,128]{1,0:T(8,128)S(1)} %collective-permute-done.2.side_ref), channel_id=1, source_target_pairs={{0,2},{1,3},{2,0},{3,1},{4,6},{5,7},{6,4},{7,5},{8,10},{9,11},{10,... | collective-permute-start | bytes 98312 | tf_op jit(solution)/shard_map/ppermute | solution.py:465
  27.7 4.0 %collective-permute-start.3 = (f32[64,128]{1,0:T(8,128)S(1)}, f32[64,128]{1,0:T(8,128)S(1)}, u32[]{:S(2)}, u32[]{:S(2)}) collective-permute-start(f32[64,128]{1,0:T(8,128)S(1)} %collective-permute-done.2.side_ref), channel_id=1, source_target_pairs={{0,254},{1,255},{2,4},{3,5},{4,2},{5,3},{6,8},{7,9},{8,6},{9,7},{1... | collective-permute-start | bytes 98312 | tf_op jit(solution)/shard_map/ppermute | solution.py:465
  39.9 7.0 %collective-permute-start.7 = (f32[56,128]{1,0:T(8,128)S(1)}, f32[56,128]{1,0:T(8,128)S(1)}, u32[]{:S(2)}, u32[]{:S(2)}) collective-permute-start(f32[56,128]{1,0:T(8,128)S(1)} %get-tuple-element.44), channel_id=1, source_target_pairs={{0,2},{2,0},{1,3},{3,1},{4,6},{6,4},{5,7},{7,5},{8,10},{10,8},{9,1... | collective-permute-start | bytes 86024 | tf_op jit(solution)/shard_map/ppermute | solution.py:417
  46.9 31.3 %copy-start = (f32[2,4,512]{2,1,0:T(4,128)S(1)}, f32[2,4,512]{2,1,0:T(4,128)}, u32[]{:S(2)}) copy-start(f32[2,4,512]{2,1,0:T(4,128)} %back_ref.1) | copy-start | bytes 49156
  74.8 3.4 %collective-permute-start.8 = (f32[56,128]{1,0:T(8,128)S(1)}, f32[56,128]{1,0:T(8,128)S(1)}, u32[]{:S(2)}, u32[]{:S(2)}) collective-permute-start(f32[56,128]{1,0:T(8,128)S(1)} %reduce_sum.19.mine_ref), channel_id=1, source_target_pairs={{0,2},{2,0},{1,3},{3,1},{4,6},{6,4},{5,7},{7,5},{8,10},{10,8},{9,1... | collective-permute-start | bytes 86024 | tf_op jit(solution)/shard_map/ppermute | solution.py:424
